TPU v7x, 8 devices: a whole 2x2x1 slice. The times are simulated.
8 devices in a mesh: fsdp: 8 (over z, y, x, core).
Axes of the slice: x: 2, y: 2, z: 1, core: 2. Of those that a mesh axis runs over, the one named last changes fastest.
Arguments:
- hidden: bfloat16 [16, 1024, 2048], P('fsdp')
- grad_out: bfloat16 [16, 1024, 2048], P('fsdp')
- positions: int32 [16, 1024], P('fsdp')
- gain_attn: bfloat16 [2048], P('fsdp')
- w_q: bfloat16 [2048, 2048], P('fsdp')
- b_q: bfloat16 [2048], P('fsdp')
- w_k: bfloat16 [2048, 2048], P('fsdp')
- b_k: bfloat16 [2048], P('fsdp')
- w_v: bfloat16 [2048, 2048], P('fsdp')
- b_v: bfloat16 [2048], P('fsdp')
- w_o: bfloat16 [2048, 2048], P('fsdp')
- gain_mlp: bfloat16 [2048], P('fsdp')
- w_gate: bfloat16 [2048, 5504], P('fsdp')
- w_up: bfloat16 [2048, 5504], P('fsdp')
- w_down: bfloat16 [5504, 2048], P('fsdp')
Outputs:
- output 1: bfloat16 [16, 1024, 2048], P('fsdp')
- output 2: bfloat16 [16, 1024, 2048], P('fsdp')
- output 3: float32 [2048], P('fsdp')
- output 4: float32 [2048, 2048], P('fsdp')
- output 5: float32 [2048], P('fsdp')
- output 6: float32 [2048, 2048], P('fsdp')
- output 7: float32 [2048], P('fsdp')
- output 8: float32 [2048, 2048], P('fsdp')
- output 9: float32 [2048], P('fsdp')
- output 10: float32 [2048, 2048], P('fsdp')
- output 11: float32 [2048], P('fsdp')
- output 12: float32 [2048, 5504], P('fsdp')
- output 13: float32 [2048, 5504], P('fsdp')
- output 14: float32 [5504, 2048], P('fsdp')
All inputs are finite; a program needn't handle non-finite values.
Results may differ from a plain program's by a relative error of at most 0.0189511.
Values are sent between devices in bfloat16 or wider.
A program may use at most 1 GiB of HBM per device.

v0:
```python
import math
import jax
import jax.numpy as jnp
from jax import lax
from jax.sharding import PartitionSpec as P

HEAD_DIM = 128
NORM_EPS = 1e-6
ROPE_THETA = 1000000.0
FSDP_AXIS = 'fsdp'


def matmul_f32(eq_form, lhs_arr, rhs_arr):
    return jnp.einsum(eq_form, lhs_arr, rhs_arr, preferred_element_type=jnp.float32)


def rope_tables(positions):
    inv_freq = 1.0 / jnp.power(ROPE_THETA, jnp.arange(0, HEAD_DIM, 2).astype(jnp.float32) / HEAD_DIM)
    angles = positions.astype(jnp.float32)[:, :, None] * inv_freq
    angles = jnp.concatenate([angles, angles], axis=-1)[:, :, None, :]
    return jnp.cos(angles), jnp.sin(angles)


def rotate_half(vec_in):
    half_dim = vec_in.shape[-1] // 2
    return jnp.concatenate([-vec_in[..., half_dim:], vec_in[..., :half_dim]], axis=-1)


def rotate_half_t(vec_in):
    half_dim = vec_in.shape[-1] // 2
    return jnp.concatenate([vec_in[..., half_dim:], -vec_in[..., :half_dim]], axis=-1)


def norm_fwd(hidden, gain_vec):
    x_f32 = hidden.astype(jnp.float32)
    inv_rms = lax.rsqrt(jnp.mean(x_f32 * x_f32, axis=-1, keepdims=True) + NORM_EPS)
    return (x_f32 * inv_rms * gain_vec.astype(jnp.float32)).astype(jnp.bfloat16), inv_rms


def norm_bwd(hidden, inv_rms, gain_vec, d_normed):
    unit_rows = hidden.astype(jnp.float32) * inv_rms
    d_gain = jnp.sum(d_normed * unit_rows, axis=(0, 1))
    d_unit = d_normed * gain_vec.astype(jnp.float32)
    d_hidden = inv_rms * (d_unit - unit_rows * jnp.mean(d_unit * unit_rows, axis=-1, keepdims=True))
    return d_hidden, d_gain


def layer_fwd(hidden, positions, weights):
    gain_attn, w_q, b_q, w_k, b_k, w_v, b_v, w_o, gain_mlp, w_gate, w_up, w_down = weights
    n_batch = hidden.shape[0]
    n_seq = hidden.shape[1]
    n_heads = w_q.shape[1] // HEAD_DIM
    n_kv = w_k.shape[1] // HEAD_DIM
    q_per_kv = n_heads // n_kv
    cos_t, sin_t = rope_tables(positions)
    normed_attn, inv_attn = norm_fwd(hidden, gain_attn)
    q_lin = (matmul_f32('bsd,de->bse', normed_attn, w_q) + b_q.astype(jnp.float32)).reshape(n_batch, n_seq, n_heads, HEAD_DIM)
    k_lin = (matmul_f32('bsd,de->bse', normed_attn, w_k) + b_k.astype(jnp.float32)).reshape(n_batch, n_seq, n_kv, HEAD_DIM)
    v_states = (matmul_f32('bsd,de->bse', normed_attn, w_v) + b_v.astype(jnp.float32)).astype(jnp.bfloat16)
    v_states = v_states.reshape(n_batch, n_seq, n_kv, HEAD_DIM)
    q_states = (q_lin * cos_t + rotate_half(q_lin) * sin_t).astype(jnp.bfloat16)
    q_states = q_states.reshape(n_batch, n_seq, n_kv, q_per_kv, HEAD_DIM)
    k_states = (k_lin * cos_t + rotate_half(k_lin) * sin_t).astype(jnp.bfloat16)
    scores = matmul_f32('bqkgd,bskd->bkgqs', q_states, k_states) / math.sqrt(HEAD_DIM)
    causal = lax.broadcasted_iota(jnp.int32, (n_seq, n_seq), 0) >= lax.broadcasted_iota(jnp.int32, (n_seq, n_seq), 1)
    attn_probs = jax.nn.softmax(jnp.where(causal, scores, -1e30), axis=-1)
    attn_out = matmul_f32('bkgqs,bskd->bqkgd', attn_probs.astype(jnp.bfloat16), v_states).astype(jnp.bfloat16)
    attn_out = attn_out.reshape(n_batch, n_seq, n_heads * HEAD_DIM)
    resid_mid = (hidden.astype(jnp.float32) + matmul_f32('bse,ed->bsd', attn_out, w_o)).astype(jnp.bfloat16)
    normed_mlp, inv_mlp = norm_fwd(resid_mid, gain_mlp)
    gate_pre = matmul_f32('bsd,df->bsf', normed_mlp, w_gate)
    up_proj = matmul_f32('bsd,df->bsf', normed_mlp, w_up)
    act_mlp = (jax.nn.silu(gate_pre) * up_proj).astype(jnp.bfloat16)
    layer_out = (resid_mid.astype(jnp.float32) + matmul_f32('bsf,fd->bsd', act_mlp, w_down)).astype(jnp.bfloat16)
    saved_acts = {'cos_t': cos_t, 'sin_t': sin_t, 'normed_attn': normed_attn, 'inv_attn': inv_attn, 'q_states': q_states, 'k_states': k_states, 'v_states': v_states, 'attn_probs': attn_probs, 'attn_out': attn_out, 'resid_mid': resid_mid, 'normed_mlp': normed_mlp, 'inv_mlp': inv_mlp, 'gate_pre': gate_pre, 'up_proj': up_proj, 'act_mlp': act_mlp}
    return layer_out, saved_acts


def layer_bwd(hidden, grad_out, saved_acts, weights):
    gain_attn, w_q, b_q, w_k, b_k, w_v, b_v, w_o, gain_mlp, w_gate, w_up, w_down = weights
    n_batch = hidden.shape[0]
    n_seq = hidden.shape[1]
    n_heads = w_q.shape[1] // HEAD_DIM
    n_kv = w_k.shape[1] // HEAD_DIM
    q_per_kv = n_heads // n_kv
    cos_t = saved_acts['cos_t']
    sin_t = saved_acts['sin_t']
    d_w_down = matmul_f32('bsf,bsd->fd', saved_acts['act_mlp'], grad_out)
    d_act = matmul_f32('bsd,fd->bsf', grad_out, w_down).astype(jnp.bfloat16).astype(jnp.float32)
    gate_pre = saved_acts['gate_pre']
    gate_sig = jax.nn.sigmoid(gate_pre)
    d_gate = (d_act * saved_acts['up_proj'] * gate_sig * (1.0 + gate_pre * (1.0 - gate_sig))).astype(jnp.bfloat16)
    d_up = (d_act * gate_pre * gate_sig).astype(jnp.bfloat16)
    normed_mlp = saved_acts['normed_mlp']
    d_w_gate = matmul_f32('bsd,bsf->df', normed_mlp, d_gate)
    d_w_up = matmul_f32('bsd,bsf->df', normed_mlp, d_up)
    d_normed_mlp = (matmul_f32('bsf,df->bsd', d_gate, w_gate) + matmul_f32('bsf,df->bsd', d_up, w_up)).astype(jnp.bfloat16).astype(jnp.float32)
    d_resid_norm, d_gain_mlp = norm_bwd(saved_acts['resid_mid'], saved_acts['inv_mlp'], gain_mlp, d_normed_mlp)
    d_resid = (grad_out.astype(jnp.float32) + d_resid_norm).astype(jnp.bfloat16)
    d_w_o = matmul_f32('bse,bsd->ed', saved_acts['attn_out'], d_resid)
    d_attn = matmul_f32('bsd,ed->bse', d_resid, w_o).astype(jnp.bfloat16).reshape(n_batch, n_seq, n_kv, q_per_kv, HEAD_DIM)
    attn_probs = saved_acts['attn_probs']
    d_v_states = matmul_f32('bkgqs,bqkgd->bskd', attn_probs.astype(jnp.bfloat16), d_attn).astype(jnp.bfloat16)
    d_probs = matmul_f32('bqkgd,bskd->bkgqs', d_attn, saved_acts['v_states'])
    d_scores = (attn_probs * (d_probs - jnp.sum(attn_probs * d_probs, axis=-1, keepdims=True)) / math.sqrt(HEAD_DIM)).astype(jnp.bfloat16)
    d_q_rot = matmul_f32('bkgqs,bskd->bqkgd', d_scores, saved_acts['k_states']).astype(jnp.bfloat16).astype(jnp.float32)
    d_q_rot = d_q_rot.reshape(n_batch, n_seq, n_heads, HEAD_DIM)
    d_k_rot = matmul_f32('bkgqs,bqkgd->bskd', d_scores, saved_acts['q_states']).astype(jnp.bfloat16).astype(jnp.float32)
    d_q_lin = (d_q_rot * cos_t + rotate_half_t(d_q_rot * sin_t)).reshape(n_batch, n_seq, n_heads * HEAD_DIM)
    d_k_lin = (d_k_rot * cos_t + rotate_half_t(d_k_rot * sin_t)).reshape(n_batch, n_seq, n_kv * HEAD_DIM)
    d_v_lin = d_v_states.reshape(n_batch, n_seq, n_kv * HEAD_DIM)
    d_b_q = jnp.sum(d_q_lin, axis=(0, 1))
    d_b_k = jnp.sum(d_k_lin, axis=(0, 1))
    d_b_v = jnp.sum(d_v_lin.astype(jnp.float32), axis=(0, 1))
    d_q_bf = d_q_lin.astype(jnp.bfloat16)
    d_k_bf = d_k_lin.astype(jnp.bfloat16)
    normed_attn = saved_acts['normed_attn']
    d_w_q = matmul_f32('bsd,bse->de', normed_attn, d_q_bf)
    d_w_k = matmul_f32('bsd,bse->de', normed_attn, d_k_bf)
    d_w_v = matmul_f32('bsd,bse->de', normed_attn, d_v_lin)
    d_normed_attn = (matmul_f32('bse,de->bsd', d_q_bf, w_q) + matmul_f32('bse,de->bsd', d_k_bf, w_k) + matmul_f32('bse,de->bsd', d_v_lin, w_v)).astype(jnp.bfloat16).astype(jnp.float32)
    d_hidden_norm, d_gain_attn = norm_bwd(hidden, saved_acts['inv_attn'], gain_attn, d_normed_attn)
    grad_hidden = (d_resid.astype(jnp.float32) + d_hidden_norm).astype(jnp.bfloat16)
    grad_list = (d_gain_attn, d_w_q, d_b_q, d_w_k, d_b_k, d_w_v, d_b_v, d_w_o, d_gain_mlp, d_w_gate, d_w_up, d_w_down)
    return grad_hidden, grad_list


def gather_all(shards):
    return tuple(lax.all_gather(w_shard, FSDP_AXIS, axis=0, tiled=True) for w_shard in shards)


def solution(mesh):
    act_spec = P(FSDP_AXIS, None, None)
    mat_spec = P(FSDP_AXIS, None)
    vec_spec = P(FSDP_AXIS)
    param_specs = (vec_spec, mat_spec, vec_spec, mat_spec, vec_spec, mat_spec, vec_spec, mat_spec, vec_spec, mat_spec, mat_spec, mat_spec)
    in_specs_all = (act_spec, act_spec, mat_spec) + param_specs
    out_specs_all = (act_spec, act_spec) + param_specs

    def local_step(hidden, grad_out, positions, *shards):
        full_fwd = gather_all(shards)
        layer_out, saved_acts = layer_fwd(hidden, positions, full_fwd)
        shards_bwd, saved_acts = lax.optimization_barrier((shards, saved_acts))
        full_bwd = gather_all(shards_bwd)
        grad_hidden, grad_list = layer_bwd(hidden, grad_out, saved_acts, full_bwd)
        grad_shards = tuple(lax.psum_scatter(grad_part, FSDP_AXIS, scatter_dimension=0, tiled=True) for grad_part in grad_list)
        return (layer_out, grad_hidden) + grad_shards

    return jax.shard_map(local_step, mesh=mesh, in_specs=in_specs_all, out_specs=out_specs_all, check_vma=False)
```

profile of v0, /device:TPU:0, one launch (start us, length us, event | category | flops | bytes accessed | tf_op | source)
XLA Modules:
  0.0 2581.1 jit_solution(7828512505010256877)
XLA Ops:
  252.1 61.9 %fusion.6 = (f32[2,16,1024]{2,1,0:T(8,128)S(1)}, f32[2,16,1024,1024]{3,2,1,0:T(8,128)}) fusion(pred[1024,1024]{0,1:T(8,128)(4,1)S(1)} %copy-done, bf16[2,1024,16,128]{1,3,2,0:T(8,128)(2,1)} %fusion.56, f32[2,1024,16,64]{1,3,2,0:T(8,128)} %get-tuple-element.83, f32[2,1024,16,64]{1,3,2,0:T(8,128)} %get-tuple-element.84, f32[2,1024,16,128]{1,3,2,0:T(8,128)} %bitcast.263, ...), kind=kOutput, calls=%fused_computation.10 | convolution fusion | flops 8711536640 | bytes 179437568 | tf_op jit(solution)/shard_map/bqkgd,bskd->bkgqs/dot_general | solution.py:14
  314.0 44.2 %fusion.5 = f32[2,16,1024]{2,1,0:T(8,128)S(1)} fusion(f32[2,16,1024,1024]{3,2,1,0:T(8,128)} %get-tuple-element.100, f32[2,16,1024]{2,1,0:T(8,128)S(1)} %get-tuple-element.99, pred[1024,1024]{0,1:T(8,128)(4,1)S(1)} %copy-done), kind=kLoop, calls=%fused_computation.9 | loop fusion | flops 134184960 | bytes 135528448 | tf_op jit(solution)/shard_map/reduce_sum | solution.py:66
  358.2 89.5 %fusion.4 = f32[2,16,1,1024,1024]{3,4,1,0,2:T(8,128)} fusion(f32[2,16,1024,1024]{3,2,1,0:T(8,128)} %get-tuple-element.100, f32[2,16,1024]{2,1,0:T(8,128)S(1)} %fusion.5, f32[2,16,1024]{2,1,0:T(8,128)S(1)} %get-tuple-element.99, pred[1024,1024]{0,1:T(8,128)(4,1)S(1)} %copy-done), kind=kLoop, calls=%fused_computation.8 | loop fusion | flops 134217728 | bytes 269746176 | tf_op jit(solution)/shard_map/div | solution.py:66
  447.7 47.3 %fusion.106 = bf16[2,16,128,1024]{3,2,1,0:T(8,128)(2,1)} fusion(f32[2,16,1,1024,1024]{3,4,1,0,2:T(8,128)} %fusion.4, bf16[2,1024,2048]{2,1,0:T(8,128)(2,1)} %add_convert_fusion.3), kind=kOutput, calls=%fused_computation.138 | convolution fusion | flops 8627683328 | bytes 150994944 | tf_op jit(solution)/shard_map/bkgqs,bskd->bqkgd/dot_general | solution.py:14
  545.9 58.3 %fusion.32 = f32[2,1024,5504]{2,1,0:T(8,128)} fusion(bf16[2,1024,2048]{2,1,0:T(8,128)(2,1)} %fusion.49, bf16[2048,5504]{1,0:T(8,128)(2,1)} %all-gather.30.cloned.1.call-done), kind=kOutput, calls=%fused_computation.50 | convolution fusion | flops 46170898432 | bytes 76021760 | tf_op jit(solution)/shard_map/bsd,df->bsf/dot_general | solution.py:14
  604.2 63.0 %multiply_convert_fusion = (bf16[2,1024,5504]{2,1,0:T(8,128)(2,1)}, f32[2,1024,5504]{2,1,0:T(8,128)}) fusion(f32[2,1024,5504]{2,1,0:T(8,128)} %fusion.32, bf16[2,1024,2048]{2,1,0:T(8,128)(2,1)} %fusion.49, bf16[2048,5504]{1,0:T(8,128)(2,1)} %all-gather.32.cloned.1.call-done), kind=kOutput, calls=%fused_computation.26 | convolution fusion | flops 46238531584 | bytes 143654912 | tf_op jit(solution)/shard_map/bsd,df->bsf/dot_general | solution.py:14
  682.9 94.1 %all-gather.36.cloned.1.call-done = bf16[5504,2048]{1,0:T(8,128)(2,1)} async-done(((bf16[688,2048]{1,0:T(8,128)(2,1)}), bf16[5504,2048]{1,0:T(8,128)(2,1)}) %all-gather.36.cloned.1.call-update) | async-done | bytes 22544400 | tf_op jit(solution)/shard_map/all_gather | solution.py:129
  777.0 97.9 %fusion.16 = (bf16[2,1024,5504]{2,1,0:T(8,128)(2,1)}, bf16[2,1024,5504]{2,1,0:T(8,128)(2,1)}) fusion(f32[2,1024,5504]{2,1,0:T(8,128)} %get-tuple-element.40, f32[2,1024,5504]{2,1,0:T(8,128)} %fusion.32, bf16[2,1024,2048]{2,1,0:T(8,128)(2,1)} %param.16, bf16[5504,2048]{1,0:T(8,128)(2,1)} %all-gather.36.cloned.1.call-done), kind=kOutput, calls=%fused_computation.22 | convolution fusion | flops 46339981312 | bytes 166199296 | tf_op jit(solution)/shard_map/bsd,fd->bsf/dot_general | solution.py:14
  887.4 62.7 %fusion.22 = f32[2,1024,2048]{2,1,0:T(8,128)} fusion(bf16[2,1024,5504]{2,1,0:T(8,128)(2,1)} %get-tuple-element.74, bf16[2048,5504]{1,0:T(8,128)(2,1)} %all-gather.40.cloned.1.call-done), kind=kOutput, calls=%fused_computation.40 | convolution fusion | flops 46170898432 | bytes 61865984 | tf_op jit(solution)/shard_map/bsf,df->bsd/dot_general | solution.py:14
  950.1 47.7 %all-gather.38.cloned.1.call-done = bf16[2048,5504]{1,0:T(8,128)(2,1)} async-done(((bf16[256,5504]{1,0:T(8,128)(2,1)}), bf16[2048,5504]{1,0:T(8,128)(2,1)}) %all-gather.38.cloned.1.call-update) | async-done | bytes 22544400 | tf_op jit(solution)/shard_map/all_gather | solution.py:129
  997.8 68.2 %fusion.44 = (f32[2048]{0:T(1024)}, f32[2,1024]{1,0:T(2,128)S(1)}, bf16[2,1024,2048]{2,1,0:T(8,128)(2,1)}) fusion(bf16[2,1024,2048]{2,1,0:T(8,128)(2,1)} %get-tuple-element.45, f32[2,1024]{1,0:T(2,128)S(1)} %bitcast.288, f32[2048]{0:T(1024)S(1)} %bitcast.292, f32[2,1024,2048]{2,1,0:T(8,128)} %fusion.22, bf16[2,1024,5504]{2,1,0:T(8,128)(2,1)} %get-tuple-element.73, ...), kind=kOutput, calls=%fused_computation.65 | convolution fusion | flops 46212841472 | bytes 78675968 | tf_op jit(solution)/shard_map/bsf,df->bsd/dot_general | solution.py:14
  1137.1 51.3 %convert_reduce_fusion = (f32[16,128]{1,0:T(8,128)}, bf16[2,16,128,1024]{3,2,1,0:T(8,128)(2,1)}) fusion(bf16[2,1024,16,128]{1,3,2,0:T(8,128)(2,1)} %bitcast.267, f32[2,16,1,1024,1024]{3,4,1,0,2:T(8,128)} %fusion.4), kind=kOutput, calls=%fused_computation.93 | convolution fusion | flops 8636069888 | bytes 151003136 | tf_op jit(solution)/shard_map/bkgqs,bqkgd->bskd/dot_general | solution.py:14
  1212.9 94.9 %fusion = (f32[2,16,1024]{2,1,0:T(8,128)S(1)}, f32[2,16,1024,1024]{3,2,1,0:T(8,128)}) fusion(f32[2,16,1,1024,1024]{3,4,1,0,2:T(8,128)} %fusion.4, bf16[2,1024,16,128]{1,3,2,0:T(8,128)(2,1)} %bitcast.268, bf16[2,1024,16,128]{3,2,1,0:T(8,128)(2,1)} %bitcast.272), kind=kOutput, calls=%fused_computation.3 | convolution fusion | flops 8657010688 | bytes 285343744 | tf_op jit(solution)/shard_map/bqkgd,bskd->bkgqs/dot_general | solution.py:14
  1307.9 115.6 %fusion.7 = bf16[2,16,1024,1024]{2,3,1,0:T(8,128)(2,1)} fusion(f32[2,16,1,1024,1024]{3,4,1,0,2:T(8,128)} %fusion.4, f32[2,16,1024,1024]{3,2,1,0:T(8,128)} %get-tuple-element.107, f32[2,16,1024]{2,1,0:T(8,128)S(1)} %get-tuple-element.106), kind=kLoop, calls=%fused_computation.11 | loop fusion | flops 134217728 | bytes 335675392 | tf_op jit(solution)/shard_map/reshape.9
  1423.5 41.0 %bitcast_convert_fusion = (f32[2,16,128,1,1024]{4,2,1,0,3:T(8,128)}, bf16[2,16,128,1024]{3,2,1,0:T(8,128)(2,1)}) fusion(bf16[2,1024,16,128]{1,3,2,0:T(8,128)(2,1)} %fusion.56, bf16[2,16,1024,1024]{2,3,1,0:T(8,128)(2,1)} %fusion.7), kind=kOutput, calls=%fused_computation.119 | convolution fusion | flops 8598323200 | bytes 100663296 | tf_op jit(solution)/shard_map/bkgqs,bskd->bqkgd/dot_general | solution.py:14
  1464.5 47.0 %bitcast_multiply_fusion.5 = (f32[2,1024,16,128]{1,3,2,0:T(8,128)}, f32[2,1024,16,128]{1,3,2,0:T(8,128)}, bf16[2,16,128,1024]{3,2,1,0:T(8,128)(2,1)}) fusion(f32[2,1024,128]{1,2,0:T(8,128)S(1)} %bitcast.274, bf16[2,16,128,1024]{3,2,1,0:T(8,128)(2,1)} %get-tuple-element.110, bf16[2,16,1024,1024]{2,3,1,0:T(8,128)(2,1)} %fusion.7, ...), kind=kOutput, calls=%fused_computation.91 | convolution fusion | flops 8610906112 | bytes 126877696 | tf_op jit(solution)/shard_map/bkgqs,bqkgd->bskd/dot_general | solution.py:14
  1535.2 26.9 %fusion.92 = (f32[16,128]{1,0:T(8,128)}, f32[16,128]{1,0:T(8,128)}, bf16[2,1024,16,128]{1,3,2,0:T(8,128)(2,1)}, f32[2,1024,16,128]{1,3,2,0:T(8,128)}) fusion(f32[2,1024,16,64]{1,3,2,0:T(8,128)} %get-tuple-element.78, f32[2,1024,16,64]{1,3,2,0:T(8,128)} %get-tuple-element.77, f32[2,1024,128]{1,2,0:T(8,128)S(1)} %bitcast.275, ...), kind=kLoop, calls=%fused_computation.136 | loop fusion | flops 46133248 | bytes 76562432 | tf_op jit(solution)/shard_map/reduce_sum | solution.py:113
  1696.0 58.0 %convolution_bitcast_fusion = f32[5504,2048]{1,0:T(8,128)} fusion(bf16[2,1024,5504]{2,1,0:T(8,128)(2,1)} %get-tuple-element.61, bf16[2,1024,2048]{2,1,0:T(8,128)(2,1)} %param.16), kind=kOutput, calls=%fused_computation.31 | convolution fusion | flops 46170898432 | bytes 76021760 | tf_op jit(solution)/shard_map/bsf,bsd->fd/dot_general | solution.py:14
  1754.0 59.4 %convolution_bitcast_fusion.1 = f32[2048,5504]{1,0:T(8,128)} fusion(bf16[2,1024,2048]{2,1,0:T(8,128)(2,1)} %fusion.49, bf16[2,1024,5504]{2,1,0:T(8,128)(2,1)} %get-tuple-element.74), kind=kOutput, calls=%fused_computation.32 | convolution fusion | flops 46170898432 | bytes 76021760 | tf_op jit(solution)/shard_map/bsd,bsf->df/dot_general | solution.py:14
  1813.5 62.4 %convolution_bitcast_fusion.2 = f32[2048,5504]{1,0:T(8,128)} fusion(bf16[2,1024,2048]{2,1,0:T(8,128)(2,1)} %fusion.49, bf16[2,1024,5504]{2,1,0:T(8,128)(2,1)} %get-tuple-element.73), kind=kOutput, calls=%fused_computation.33 | convolution fusion | flops 46170898432 | bytes 76021760 | tf_op jit(solution)/shard_map/bsd,bsf->df/dot_general | solution.py:14
  1887.8 57.6 %fusion.50 = bf16[2,1024,2048]{2,1,0:T(8,128)(2,1)} fusion(bf16[2,1024,2048]{2,1,0:T(8,128)(2,1)} %get-tuple-element.45, bf16[2,1024,5504]{2,1,0:T(8,128)(2,1)} %get-tuple-element.61, bf16[5504,2048]{1,0:T(8,128)(2,1)} %all-gather.34.cloned.1.call-done), kind=kOutput, calls=%fused_computation.71 | convolution fusion | flops 46183481344 | bytes 61865984 | tf_op jit(solution)/shard_map/bsf,fd->bsd/dot_general | solution.py:14
  1995.2 34.6 %fusion.46 = (f32[2048]{0:T(1024)S(1)}, f32[2,1024]{1,0:T(2,128)S(1)}, bf16[2,1024,2048]{2,1,0:T(8,128)(2,1)}) fusion(bf16[2,1024,2048]{2,1,0:T(8,128)(2,1)} %param.15, f32[2,1024]{1,0:T(2,128)S(1)} %bitcast.285, f32[2048]{0:T(1024)S(1)} %bitcast.290, f32[2,1024,2048]{2,1,0:T(8,128)} %fusion.70, f32[2,1024,2048]{2,1,0:T(8,128)} %fusion.76, ...), kind=kOutput, calls=%fused_computation.67 | convolution fusion | flops 17226002432 | bytes 67141632 | tf_op jit(solution)/shard_map/bse,de->bsd/dot_general | solution.py:14
  2070.9 248.0 %reduce-scatter.18.cloned.1.call-done = f32[256,5504]{1,0:T(8,128)} async-done(((f32[2048,5504]{1,0:T(8,128)}), f32[256,5504]{1,0:T(8,128)}) %reduce-scatter.18.cloned.1.call-update) | async-done | bytes 5636112 | tf_op jit(solution)/shard_map/reduce_scatter | solution.py:146
  2318.9 255.1 %reduce-scatter.16.cloned.1.call-done = f32[256,5504]{1,0:T(8,128)} async-done(((f32[2048,5504]{1,0:T(8,128)}), f32[256,5504]{1,0:T(8,128)}) %reduce-scatter.16.cloned.1.call-update) | async-done | bytes 5636112 | tf_op jit(solution)/shard_map/reduce_scatter | solution.py:146
  (180 shorter events, 679.5 us)
Async XLA Ops:
  7.2 81.6 %all-gather.24.cloned.1.call-start = ((), (), s32[]{:S(2)}) async-start(), calls=%async_computation.8 | async-start | bytes 9437184 | tf_op jit(solution)/shard_map/all_gather | solution.py:129
  8.0 135.2 %all-gather.26.cloned.1.call-start = ((), (), s32[]{:S(2)}) async-start(), calls=%async_computation.9 | async-start | bytes 9437184 | tf_op jit(solution)/shard_map/all_gather | solution.py:129
  8.7 194.4 %all-gather.22.cloned.1.call-start = ((), (), s32[]{:S(2)}) async-start(), calls=%async_computation.7 | async-start | bytes 9437184 | tf_op jit(solution)/shard_map/all_gather | solution.py:129
  9.5 485.6 %all-gather.28.cloned.1.call-start = ((), (), s32[]{:S(2)}) async-start(), calls=%async_computation.10 | async-start | bytes 9437184 | tf_op jit(solution)/shard_map/all_gather | solution.py:129
  10.0 535.8 %all-gather.30.cloned.1.call-start = ((), (), s32[]{:S(2)}) async-start(), calls=%async_computation.11 | async-start | bytes 25362432 | tf_op jit(solution)/shard_map/all_gather | solution.py:129
  10.6 593.5 %all-gather.32.cloned.1.call-start = ((), (), s32[]{:S(2)}) async-start(), calls=%async_computation.12 | async-start | bytes 25362432 | tf_op jit(solution)/shard_map/all_gather | solution.py:129
  11.2 765.8 %all-gather.36.cloned.1.call-start = ((), (), s32[]{:S(2)}) async-start(), calls=%async_computation.14 | async-start | bytes 25362432 | tf_op jit(solution)/shard_map/all_gather | solution.py:129
  604.2 67.2 %copy-start.24 = (bf16[256]{0:T(256)(128)(2,1)S(1)}, bf16[256]{0:T(256)(128)(2,1)}, u32[]{:S(2)}) copy-start(bf16[256]{0:T(256)(128)(2,1)} %param.26) | copy-start | bytes 1540
  667.2 220.2 %all-gather.40.cloned.1.call-start = ((), (), s32[]{:S(2)}) async-start(), calls=%async_computation.16 | async-start | bytes 25362432 | tf_op jit(solution)/shard_map/all_gather | solution.py:129
  668.0 329.8 %all-gather.38.cloned.1.call-start = ((), (), s32[]{:S(2)}) async-start(), calls=%async_computation.15 | async-start | bytes 25362432 | tf_op jit(solution)/shard_map/all_gather | solution.py:129
  668.7 432.3 %all-gather.42.cloned.1.call-start = ((), (), s32[]{:S(2)}) async-start(), calls=%async_computation.17 | async-start | bytes 9437184 | tf_op jit(solution)/shard_map/all_gather | solution.py:129
  669.3 1218.5 %all-gather.34.cloned.1.call-start = ((), (), s32[]{:S(2)}) async-start(), calls=%async_computation.13 | async-start | bytes 25362432 | tf_op jit(solution)/shard_map/all_gather | solution.py:129
  670.0 1275.4 %all-gather.44.cloned.1.call-start = ((), (), s32[]{:S(2)}) async-start(), calls=%async_computation.18 | async-start | bytes 9437184 | tf_op jit(solution)/shard_map/all_gather | solution.py:129
  670.6 1299.6 %all-gather.48.cloned.1.call-start = ((), (), s32[]{:S(2)}) async-start(), calls=%async_computation.20 | async-start | bytes 9437184 | tf_op jit(solution)/shard_map/all_gather | solution.py:129
  671.4 1323.8 %all-gather.46.cloned.1.call-start = ((), (), s32[]{:S(2)}) async-start(), calls=%async_computation.19 | async-start | bytes 9437184 | tf_op jit(solution)/shard_map/all_gather | solution.py:129
  682.8 1388.0 %reduce-scatter.14.cloned.1.call-start = ((), (), s32[]{:S(2)}) async-start(), calls=%async_computation.24 | async-start | bytes 18874368 | tf_op jit(solution)/shard_map/reduce_scatter | solution.py:146
  887.4 110.4 %copy-start.13 = (f32[2,1024,1]{1,0,2:T(2,128)S(1)}, f32[2,1024,1]{1,0,2:T(2,128)}, u32[]{:S(2)}) copy-start(f32[2,1024,1]{1,0,2:T(2,128)} %get-tuple-element.38) | copy-start | bytes 24580
  887.4 110.4 %copy-start.15 = (f32[8,1,256]{2,1,0:T(1,128)S(1)}, f32[8,1,256]{2,1,0:T(1,128)}, u32[]{:S(2)}) copy-start(f32[8,1,256]{2,1,0:T(1,128)} %convert_element_type.244) | copy-start | bytes 24580
  1101.0 969.9 %reduce-scatter.12.cloned.1.call-start = ((), (), s32[]{:S(2)}) async-start(), calls=%async_computation.23 | async-start | bytes 18874368 | tf_op jit(solution)/shard_map/reduce_scatter | solution.py:146
  1307.8 763.1 %reduce-scatter.10.cloned.1.call-start = ((), (), s32[]{:S(2)}) async-start(), calls=%async_computation.22 | async-start | bytes 18874368 | tf_op jit(solution)/shard_map/reduce_scatter | solution.py:146
  1586.6 484.3 %reduce-scatter.8.cloned.1.call-start = ((), (), s32[]{:S(2)}) async-start(), calls=%async_computation.21 | async-start | bytes 18874368 | tf_op jit(solution)/shard_map/reduce_scatter | solution.py:146
  1695.5 375.4 %reduce-scatter.20.cloned.1.call-start = ((), (), s32[]{:S(2)}) async-start(), calls=%async_computation.27 | async-start | bytes 50724864 | tf_op jit(solution)/shard_map/reduce_scatter | solution.py:146
  1754.0 564.9 %reduce-scatter.18.cloned.1.call-start = ((), (), s32[]{:S(2)}) async-start(), calls=%async_computation.26 | async-start | bytes 50724864 | tf_op jit(solution)/shard_map/reduce_scatter | solution.py:146
  1813.4 760.6 %reduce-scatter.16.cloned.1.call-start = ((), (), s32[]{:S(2)}) async-start(), calls=%async_computation.25 | async-start | bytes 50724864 | tf_op jit(solution)/shard_map/reduce_scatter | solution.py:146
  (24 other events, 567.6 us)
Sparse Core Ops, SparseCore 0:
  9.9 51.5 all-gather.23
  63.3 48.6 all-gather.25
  113.8 48.6 all-gather.21
  164.2 48.6 all-gather.27
  214.6 108.5 all-gather.29
  324.9 108.5 all-gather.31
  667.3 109.6 all-gather.35
  778.8 108.5 all-gather.39
  889.2 108.5 all-gather.37
  999.5 48.6 all-gather.41
  1050.0 108.5 all-gather.33
  1160.3 48.6 all-gather.43
  1210.8 48.6 all-gather.47
  1261.2 48.6 all-gather.45
  1313.9 107.8 reduce-scatter.13
  1425.7 107.8 reduce-scatter.11
  1586.7 108.7 reduce-scatter.9
  1699.4 107.8 reduce-scatter.7
  1811.5 252.3 reduce-scatter.19
  2068.0 250.8 reduce-scatter.17
  2323.2 250.8 reduce-scatter.15
where the time goes:
time: 2590 us; the launch traced here: 2580 us
  matrix products  1230 us (47%)
  waiting for transfers between devices  665 us (26%)
  other arithmetic  438 us (17%)
  local copies, waits for them, and re-layouts  133 us (5%)
  blocking collectives  97.3 us (4%)
    dot_general x27, matrix products, matmul_f32(): jnp.einsum(eq_form, lhs_arr, rhs_arr, preferred_element_type=jnp.float32)  1230 us
    reduce_scatter x7, waiting for transfers between devices, local_step(): lax.psum_scatter(grad_part, FSDP_AXIS, scatter_dimension=0, tiled=True)  503 us
    all_gather x14, waiting for transfers between devices, gather_all(): lax.all_gather(w_shard, FSDP_AXIS, axis=0, tiled=True)  154 us
    another operation x1, other arithmetic  116 us
    div x1, other arithmetic, layer_fwd(): attn_probs = jax.nn.softmax(jnp.where(causal, scores, -1e+30), axis=-1)  89.5 us
    all_gather x7, blocking collectives, gather_all(): lax.all_gather(w_shard, FSDP_AXIS, axis=0, tiled=True)  73 us
  transfers between devices with their start and end apart: 21, of which 5 were waited for; matrix products, arithmetic and copies ran while one was open for 67% of the time, Pallas kernels for 0%

commit v1 on v0

v1 whole, which is shorter than its diff:
```python
import math
import jax
import jax.numpy as jnp
import numpy as np
from jax import lax
from jax.experimental import pallas as pl
from jax.experimental.pallas import tpu as pltpu
from jax.sharding import Mesh, PartitionSpec as P

HEAD_DIM = 128
NORM_EPS = 1e-6
ROPE_THETA = 1000000.0
BLOCK_Q = 256
SCALE = 1.0 / math.sqrt(HEAD_DIM)
ALL = ('chip', 'core')
BF16 = jnp.bfloat16
F32 = jnp.float32


def mm(lhs, rhs):
    return lax.dot_general(lhs, rhs, (((1,), (0,)), ((), ())), preferred_element_type=F32)


def mm_nt(lhs, rhs):
    return lax.dot_general(lhs, rhs, (((1,), (1,)), ((), ())), preferred_element_type=F32)


def mm_tn(lhs, rhs):
    return lax.dot_general(lhs, rhs, (((0,), (0,)), ((), ())), preferred_element_type=F32)


def rope_tables(positions):
    inv_freq = 1.0 / jnp.power(ROPE_THETA, jnp.arange(0, HEAD_DIM, 2).astype(F32) / HEAD_DIM)
    angles = positions.astype(F32)[:, :, None] * inv_freq
    cos_h, sin_h = jnp.cos(angles), jnp.sin(angles)
    return jnp.concatenate([cos_h, cos_h], axis=-1), jnp.concatenate([-sin_h, sin_h], axis=-1)


def swap_halves(vec):
    return pltpu.roll(vec, HEAD_DIM // 2, 1)


def softmax_rows(scores, row0):
    n_rows, n_keys = scores.shape
    row_id = row0 + lax.broadcasted_iota(jnp.int32, (n_rows, n_rows), 0)
    col_id = (n_keys - n_rows) + lax.broadcasted_iota(jnp.int32, (n_rows, n_rows), 1)
    diag = jnp.where(row_id >= col_id, scores[:, n_keys - n_rows:], -1e30)
    if n_keys > n_rows:
        scores = jnp.concatenate([scores[:, :n_keys - n_rows], diag], axis=1)
    else:
        scores = diag
    top = jnp.max(scores, axis=1, keepdims=True)
    expd = jnp.exp((scores - top) * SCALE)
    return expd * (1.0 / jnp.sum(expd, axis=1, keepdims=True))


def attn_fwd_kernel(qkv_ref, cos_ref, sin_ref, o_ref, rot_ref):
    cos_t, sin_t = cos_ref[0], sin_ref[0]
    for part in range(2):
        lin = qkv_ref[0, :, part * HEAD_DIM:(part + 1) * HEAD_DIM]
        rot_ref[0, :, part * HEAD_DIM:(part + 1) * HEAD_DIM] = (lin * cos_t + swap_halves(lin) * sin_t).astype(BF16)
    rot_ref[0, :, 2 * HEAD_DIM:] = qkv_ref[0, :, 2 * HEAD_DIM:].astype(BF16)
    n_seq = qkv_ref.shape[1]
    for row0 in range(0, n_seq, BLOCK_Q):
        n_keys = row0 + BLOCK_Q
        q_blk = rot_ref[0, row0:n_keys, :HEAD_DIM]
        k_blk = rot_ref[0, :n_keys, HEAD_DIM:2 * HEAD_DIM]
        v_blk = rot_ref[0, :n_keys, 2 * HEAD_DIM:]
        probs = softmax_rows(mm_nt(q_blk, k_blk), row0)
        o_ref[0, row0:n_keys, :] = mm(probs.astype(BF16), v_blk).astype(BF16)


def attn_bwd_kernel(rot_ref, do_ref, cos_ref, sin_ref, dqkv_ref, dbias_ref, dk_acc, dv_acc):
    n_seq = rot_ref.shape[1]
    cos_t, sin_t = cos_ref[0], sin_ref[0]
    dbias_q = jnp.zeros((1, HEAD_DIM), F32)
    for row0 in reversed(range(0, n_seq, BLOCK_Q)):
        n_keys = row0 + BLOCK_Q
        q_blk = rot_ref[0, row0:n_keys, :HEAD_DIM]
        k_blk = rot_ref[0, :n_keys, HEAD_DIM:2 * HEAD_DIM]
        v_blk = rot_ref[0, :n_keys, 2 * HEAD_DIM:]
        do_blk = do_ref[0, row0:n_keys, :]
        probs = softmax_rows(mm_nt(q_blk, k_blk), row0)
        d_probs = mm_nt(do_blk, v_blk)
        delta = jnp.sum(probs * d_probs, axis=1, keepdims=True)
        d_scores = (probs * (d_probs - delta) * SCALE).astype(BF16)
        dv_part = mm_tn(probs.astype(BF16), do_blk)
        dk_part = mm_tn(d_scores, q_blk)
        if n_keys == n_seq:
            dv_acc[...] = dv_part
            dk_acc[...] = dk_part
        else:
            dv_acc[:n_keys] += dv_part
            dk_acc[:n_keys] += dk_part
        dq_rot = mm(d_scores, k_blk).astype(BF16).astype(F32)
        dq_lin = dq_rot * cos_t[row0:n_keys] - swap_halves(dq_rot) * sin_t[row0:n_keys]
        dbias_q += jnp.sum(dq_lin, axis=0, keepdims=True)
        dqkv_ref[0, row0:n_keys, :HEAD_DIM] = dq_lin.astype(BF16)
    dk_rot = dk_acc[...].astype(BF16).astype(F32)
    dk_lin = dk_rot * cos_t - swap_halves(dk_rot) * sin_t
    dqkv_ref[0, :, HEAD_DIM:2 * HEAD_DIM] = dk_lin.astype(BF16)
    dv_lin = dv_acc[...].astype(BF16)
    dqkv_ref[0, :, 2 * HEAD_DIM:] = dv_lin
    dbias_ref[0, :, :HEAD_DIM] = dbias_q
    dbias_ref[0, :, HEAD_DIM:2 * HEAD_DIM] = jnp.sum(dk_lin, axis=0, keepdims=True)
    dbias_ref[0, :, 2 * HEAD_DIM:] = jnp.sum(dv_lin.astype(F32), axis=0, keepdims=True)


def head_spec(n_seq, width):
    return pl.BlockSpec((1, n_seq, width), lambda b, h: (b, 0, h))


def table_spec(n_seq):
    return pl.BlockSpec((1, n_seq, HEAD_DIM), lambda b, h: (b, 0, 0))


def attn_fwd(qkv_lin, cos_t, sin_t):
    n_batch, n_seq, width = qkv_lin.shape
    n_heads = width // (3 * HEAD_DIM)
    pairs = n_batch * n_heads * n_seq * (n_seq + BLOCK_Q) // 2
    return pl.pallas_call(
        attn_fwd_kernel,
        grid=(n_batch, n_heads),
        in_specs=[head_spec(n_seq, 3 * HEAD_DIM), table_spec(n_seq), table_spec(n_seq)],
        out_specs=[head_spec(n_seq, HEAD_DIM), head_spec(n_seq, 3 * HEAD_DIM)],
        out_shape=[jax.ShapeDtypeStruct((n_batch, n_seq, n_heads * HEAD_DIM), BF16), jax.ShapeDtypeStruct((n_batch, n_seq, width), BF16)],
        cost_estimate=pl.CostEstimate(flops=4 * pairs * HEAD_DIM * 2, bytes_accessed=qkv_lin.size * 6 + qkv_lin.size // 3 * 2, transcendentals=pairs),
        name='attn_fwd',
    )(qkv_lin, cos_t, sin_t)


def attn_bwd(rot, d_o, cos_t, sin_t):
    n_batch, n_seq, width = rot.shape
    n_heads = width // (3 * HEAD_DIM)
    pairs = n_batch * n_heads * n_seq * (n_seq + BLOCK_Q) // 2
    return pl.pallas_call(
        attn_bwd_kernel,
        grid=(n_batch, n_heads),
        in_specs=[head_spec(n_seq, 3 * HEAD_DIM), head_spec(n_seq, HEAD_DIM), table_spec(n_seq), table_spec(n_seq)],
        out_specs=[head_spec(n_seq, 3 * HEAD_DIM), pl.BlockSpec((1, 1, 3 * HEAD_DIM), lambda b, h: (b, 0, h))],
        out_shape=[jax.ShapeDtypeStruct((n_batch, n_seq, width), BF16), jax.ShapeDtypeStruct((n_batch, 1, width), F32)],
        scratch_shapes=[pltpu.VMEM((n_seq, HEAD_DIM), F32), pltpu.VMEM((n_seq, HEAD_DIM), F32)],
        cost_estimate=pl.CostEstimate(flops=10 * pairs * HEAD_DIM * 2, bytes_accessed=rot.size * 4 + rot.size // 3 * 2, transcendentals=pairs),
        name='attn_bwd',
    )(rot, d_o, cos_t, sin_t)


def norm_fwd(hidden, gain_vec):
    x_f32 = hidden.astype(F32)
    inv_rms = lax.rsqrt(jnp.mean(x_f32 * x_f32, axis=-1, keepdims=True) + NORM_EPS)
    return (x_f32 * inv_rms * gain_vec.astype(F32)).astype(BF16), inv_rms


def norm_bwd(hidden, inv_rms, gain_vec, d_normed):
    unit_rows = hidden.astype(F32) * inv_rms
    d_gain = jnp.sum(d_normed * unit_rows, axis=0)
    d_unit = d_normed * gain_vec.astype(F32)
    d_hidden = inv_rms * (d_unit - unit_rows * jnp.mean(d_unit * unit_rows, axis=-1, keepdims=True))
    return d_hidden, d_gain


def gather(shard):
    return lax.all_gather(shard, ALL, axis=0, tiled=True)


def to_partner(arr):
    return lax.ppermute(arr, 'core', [(0, 1), (1, 0)])


def after(arrs, *deps):
    n_arrs = len(arrs)
    return lax.optimization_barrier(tuple(arrs) + tuple(deps))[:n_arrs]


def split_kernel(core_ref, own_in, other_in, own_out, other_out):
    own_out[...] = own_in[...]
    other_out[...] = other_in[...]


def split_cols(core, arr, n_parts):
    n_rows, n_cols = arr.shape
    width = n_cols // n_parts
    rows = min(n_rows, 524288 // width)
    half = jax.ShapeDtypeStruct((n_rows, n_cols // 2), arr.dtype)
    out_spec = pl.BlockSpec((rows, width), lambda i, j, core_ref: (i, j))
    return pl.pallas_call(
        split_kernel,
        grid_spec=pltpu.PrefetchScalarGridSpec(
            num_scalar_prefetch=1, grid=(n_rows // rows, n_parts // 2),
            in_specs=[
                pl.BlockSpec((rows, width), lambda i, j, core_ref: (i, 2 * j + core_ref[0])),
                pl.BlockSpec((rows, width), lambda i, j, core_ref: (i, 2 * j + 1 - core_ref[0])),
            ],
            out_specs=[out_spec, out_spec],
        ),
        out_shape=[half, half],
        cost_estimate=pl.CostEstimate(flops=6 * arr.size, bytes_accessed=4 * arr.size, transcendentals=0), name='split_cols',
    )(core.reshape(1), arr, arr)


def scatter_rows(chip_sum):
    return lax.psum_scatter(chip_sum, 'chip', scatter_dimension=0, tiled=True)


def join_halves(core, rows):
    n_rows = rows.shape[0] // 2
    keep = jnp.where(core == 0, rows[:n_rows], rows[n_rows:])
    got = to_partner(jnp.where(core == 0, rows[n_rows:], rows[:n_rows]))
    return jnp.concatenate([jnp.where(core == 0, keep, got), jnp.where(core == 0, got, keep)], axis=1)


def by_head_kernel(q_ref, k_ref, v_ref, out_ref):
    for i in range(out_ref.shape[1] // HEAD_DIM):
        src = (q_ref, k_ref, v_ref)[i % 3]
        out_ref[:, i * HEAD_DIM:(i + 1) * HEAD_DIM] = src[:, i // 3 * HEAD_DIM:(i // 3 + 1) * HEAD_DIM]


def by_head(arrs):
    n_rows, n_cols = arrs[0].shape
    return pl.pallas_call(
        by_head_kernel, out_shape=jax.ShapeDtypeStruct((n_rows, 3 * n_cols), arrs[0].dtype),
        cost_estimate=pl.CostEstimate(flops=6 * arrs[0].size, bytes_accessed=12 * arrs[0].size, transcendentals=0), name='by_head',
    )(*arrs)


def from_heads_kernel(in_ref, *out_refs):
    for i in range(in_ref.shape[1] // HEAD_DIM):
        out_refs[i % 3][:, i // 3 * HEAD_DIM:(i // 3 + 1) * HEAD_DIM] = in_ref[:, i * HEAD_DIM:(i + 1) * HEAD_DIM]


def from_heads(arr):
    n_rows, n_cols = arr.shape
    block = 64
    return pl.pallas_call(
        from_heads_kernel, grid=(n_rows // block,),
        in_specs=[pl.BlockSpec((block, n_cols), lambda i: (i, 0))],
        out_specs=[pl.BlockSpec((block, n_cols // 3), lambda i: (i, 0))] * 3,
        out_shape=[jax.ShapeDtypeStruct((n_rows, n_cols // 3), arr.dtype)] * 3,
        cost_estimate=pl.CostEstimate(flops=2 * arr.size, bytes_accessed=8 * arr.size, transcendentals=0), name='from_heads',
    )(arr)


def by_head_vec(vecs):
    return jnp.concatenate([v.reshape(-1, 1, HEAD_DIM) for v in vecs], axis=1).reshape(-1)


def layer_step(hidden3, grad_out3, positions, gain_attn, w_q, b_q, w_k, b_k, w_v, b_v, w_o, gain_mlp, w_gate, w_up, w_down):
    core = lax.axis_index('core')
    n_batch, n_seq, width = hidden3.shape
    hidden = hidden3.reshape(n_batch * n_seq, width)
    grad_out = grad_out3.reshape(n_batch * n_seq, width)
    n_own = gain_attn.shape[0]
    vecs = lax.all_gather(jnp.concatenate([gain_attn, gain_mlp, by_head_vec([b_q, b_k, b_v])]), ALL, axis=0, tiled=False)
    gain_attn_f, gain_mlp_f, b_qkv = (vecs[:, lo:hi].reshape(-1) for lo, hi in ((0, n_own), (n_own, 2 * n_own), (2 * n_own, 5 * n_own)))
    w_qkv_f = gather(by_head([w_q, w_k, w_v]))
    w_o_f = gather(w_o)
    w_gate_f = gather(w_gate)
    w_up_f = gather(w_up)
    w_down_f = gather(w_down)

    gout_own, gout_other = split_cols(core, grad_out, 2)
    gout_got = to_partner(gout_other)
    cos_t, sin_t = rope_tables(positions)
    normed_attn, inv_attn = norm_fwd(hidden, gain_attn_f)
    na_own, na_other = split_cols(core, normed_attn, 8)
    na_got = to_partner(na_other)
    (normed_attn,) = after((normed_attn,), na_got, gout_got, cos_t, sin_t)
    qkv_lin = mm(normed_attn, w_qkv_f) + b_qkv.astype(F32)
    attn_out3, rot = attn_fwd(qkv_lin.reshape(n_batch, n_seq, -1), cos_t, sin_t)
    attn_out = attn_out3.reshape(n_batch * n_seq, width)
    ao_own, ao_other = split_cols(core, attn_out, 8)
    ao_got = to_partner(ao_other)
    resid_mid = (hidden.astype(F32) + mm(attn_out, w_o_f)).astype(BF16)
    normed_mlp, inv_mlp = norm_fwd(resid_mid, gain_mlp_f)
    nm_own, nm_other = split_cols(core, normed_mlp, 8)
    nm_got = to_partner(nm_other)
    (normed_mlp,) = after((normed_mlp,), nm_got, ao_got)
    gate_pre = mm(normed_mlp, w_gate_f)
    up_proj = mm(normed_mlp, w_up_f)
    act_mlp = (jax.nn.silu(gate_pre) * up_proj).astype(BF16)
    act_got = to_partner(act_mlp)

    sum_down = mm_tn(act_got, gout_got) + mm_tn(act_mlp, gout_own)
    rows_down = scatter_rows(sum_down)
    (grad_out_b,) = after((grad_out,), sum_down)
    d_act = mm_nt(grad_out_b, w_down_f).astype(BF16).astype(F32)
    gate_sig = jax.nn.sigmoid(gate_pre)
    d_gate = (d_act * up_proj * gate_sig * (1.0 + gate_pre * (1.0 - gate_sig))).astype(BF16)
    d_up = (d_act * gate_pre * gate_sig).astype(BF16)
    dg_got, du_got = to_partner(d_gate), to_partner(d_up)
    part_gate, part_up = mm_tn(nm_own, d_gate), mm_tn(nm_own, d_up)
    sum_gate = mm_tn(nm_got, dg_got) + part_gate
    sum_up = mm_tn(nm_got, du_got) + part_up
    d_w_gate, d_w_up = scatter_rows(sum_gate), scatter_rows(sum_up)
    d_gate, d_up = after((d_gate, d_up), sum_gate, sum_up)
    d_normed_mlp = (mm_nt(d_gate, w_gate_f) + mm_nt(d_up, w_up_f)).astype(BF16).astype(F32)
    d_resid_norm, d_gain_mlp = norm_bwd(resid_mid, inv_mlp, gain_mlp_f, d_normed_mlp)
    d_resid = (grad_out.astype(F32) + d_resid_norm).astype(BF16)
    dr_got = to_partner(d_resid)
    d_attn = mm_nt(d_resid, w_o_f).astype(BF16)
    sum_o = mm_tn(ao_got, dr_got) + mm_tn(ao_own, d_resid)
    d_w_o = scatter_rows(sum_o)
    (d_attn,) = after((d_attn,), sum_o)
    d_qkv3, d_bias = attn_bwd(rot, d_attn.reshape(n_batch, n_seq, width), cos_t, sin_t)
    d_qkv = d_qkv3.reshape(n_batch * n_seq, -1)
    dq_got = to_partner(d_qkv)
    sum_qkv = mm_tn(na_got, dq_got) + mm_tn(na_own, d_qkv)
    d_w_q, d_w_k, d_w_v = from_heads(scatter_rows(sum_qkv))
    d_qkv, act_mlp = after((d_qkv, act_mlp), sum_qkv)
    d_normed_attn = mm_nt(d_qkv, w_qkv_f).astype(BF16).astype(F32)
    d_hidden_norm, d_gain_attn = norm_bwd(hidden, inv_attn, gain_attn_f, d_normed_attn)
    grad_hidden = (d_resid.astype(F32) + d_hidden_norm).astype(BF16)
    layer_out = (resid_mid.astype(F32) + mm(act_mlp, w_down_f)).astype(BF16)
    d_w_down = join_halves(core, rows_down)

    d_vecs = jnp.stack([d_gain_attn, d_gain_mlp] + [jnp.sum(d_bias, axis=(0, 1)).reshape(-1, 3, HEAD_DIM)[:, j].reshape(-1) for j in range(3)])
    d_vecs = lax.all_gather(d_vecs, ALL, axis=0, tiled=False)
    me = lax.axis_index('chip') * 2 + core
    d_vecs = jnp.sum(lax.dynamic_slice_in_dim(d_vecs, me * n_own, n_own, axis=2), axis=0)
    return (
        layer_out.reshape(hidden3.shape), grad_hidden.reshape(hidden3.shape),
        d_vecs[0], d_w_q, d_vecs[2], d_w_k, d_vecs[3], d_w_v, d_vecs[4], d_w_o, d_vecs[1], d_w_gate, d_w_up, d_w_down,
    )


def solution(mesh):
    pair_mesh = Mesh(np.asarray(mesh.devices).reshape(-1, 2), ALL)
    act_spec, mat_spec, vec_spec = P(ALL, None, None), P(ALL, None), P(ALL)
    param_specs = (vec_spec, mat_spec, vec_spec, mat_spec, vec_spec, mat_spec, vec_spec, mat_spec, vec_spec, mat_spec, mat_spec, mat_spec)
    return jax.shard_map(
        layer_step, mesh=pair_mesh, in_specs=(act_spec, act_spec, mat_spec) + param_specs,
        out_specs=(act_spec, act_spec) + param_specs, check_vma=False,
    )
```

time: 2590 us -> 1880 us (0.73)
  other arithmetic: 438 us -> 69.6 us
  matrix products: 1230 us -> 881 us
  Pallas kernels: 0 us -> 243 us
  local copies, waits for them, and re-layouts: 133 us -> 1.97 us
  blocking collectives: 97.3 us -> 30 us
  waiting for transfers between devices: 665 us -> 626 us
    dot_general x27 -> x20, matrix products: 1230 us -> 881 us  [the longest x5 308 us: mm_nt(): lax.dot_general(lhs, rhs, (((1,), (1,)), ((), ())), preferred_element_typ...]
    pallas_call x0 -> x8, Pallas kernels: none -> 243 us  [the longest x1 126 us: attn_bwd(): pl.pallas_call(attn_bwd_kernel, grid=(n_batch, n_heads), in_specs=[head_s...]
    another operation x1 -> x0, other arithmetic: 116 us -> none
    div x1 -> x0, other arithmetic: 89.5 us -> none  [layer_fwd(): attn_probs = jax.nn.softmax(jnp.where(causal, scores, -1e+30), axis=-1)]
    all_gather x14 -> x5, waiting for transfers between devices: 154 us -> 80.4 us  [gather(): return lax.all_gather(shard, ALL, axis=0, tiled=True)]
    reduce_sum x2, other arithmetic: 71.1 us -> 0.09 us  [the longest x1 0.07 us: layer_step(): jnp.sum(d_bias, axis=(0, 1)).reshape(-1, 3, HEAD_DIM)[:, j].reshape(-1)]
    reshape x3 -> x2, local copies, waits for them, and re-layouts: 53.9 us -> 0.03 us  [the longest x1 0.02 us: by_head_vec(): jnp.concatenate([v.reshape(-1, 1, HEAD_DIM) for v in vecs], axis=1)]
    convert_element_type x15 -> x6, other arithmetic: 92.3 us -> 45.5 us  [the longest x2 18.6 us: norm_fwd(): return ((x_f32 * inv_rms * gain_vec.astype(F32)).astype(BF16), inv_rms)]
  transfers between devices with their start and end apart: 21 -> 20, of which waited for: 5 -> 11; matrix products, arithmetic and copies ran while one was open for 67% -> 37% of each run, Pallas kernels for 0% -> 13%
where the time goes in v1:
time: 1880 us; the launch traced here: 1870 us
  matrix products  881 us (47%)
  waiting for transfers between devices  626 us (33%)
  Pallas kernels  243 us (13%)
  other arithmetic  69.6 us (4%)
  blocking collectives  30 us (2%)
    reduce_scatter x5, waiting for transfers between devices, scatter_rows(): return lax.psum_scatter(chip_sum, 'chip', scatter_dimension=0, tiled=True)  515 us
    dot_general x5, matrix products, mm_nt(): lax.dot_general(lhs, rhs, (((1,), (1,)), ((), ())), preferred_element_typ...  308 us
    dot_general x10, matrix products, mm_tn(): lax.dot_general(lhs, rhs, (((0,), (0,)), ((), ())), preferred_element_typ...  303 us
    dot_general x5, matrix products, mm(): lax.dot_general(lhs, rhs, (((1,), (0,)), ((), ())), preferred_element_typ...  270 us
    pallas_call x1, Pallas kernels, attn_bwd(): pl.pallas_call(attn_bwd_kernel, grid=(n_batch, n_heads), in_specs=[head_s...  126 us
    all_gather x5, waiting for transfers between devices, gather(): return lax.all_gather(shard, ALL, axis=0, tiled=True)  80.4 us
    pallas_call x1, Pallas kernels, attn_fwd(): pl.pallas_call(attn_fwd_kernel, grid=(n_batch, n_heads), in_specs=[head_s...  78.6 us
  transfers between devices with their start and end apart: 20, of which 11 were waited for; matrix products, arithmetic and copies ran while one was open for 37% of the time, Pallas kernels for 13%

profile of v1, /device:TPU:0, one launch (start us, length us, event | category | flops | bytes accessed | tf_op | source)
XLA Modules:
  0.0 1869.7 jit_solution(4440602987270940517)
XLA Ops:
  67.6 66.5 %all-gather.10.cloned.1.call-done = bf16[2048,6144]{1,0:T(8,128)(2,1)} async-done(((bf16[256,6144]{1,0:T(8,128)(2,1)}), bf16[2048,6144]{1,0:T(8,128)(2,1)}) %all-gather.10.cloned.1.call-update) | async-done | bytes 25165840 | tf_op jit(solution)/shard_map/all_gather | solution.py:163
  134.1 62.8 %broadcast_add_fusion = f32[2048,6144]{1,0:T(8,128)} fusion(f32[6144]{0:T(1024)S(1)} %reshape.156, bf16[2048,2048]{1,0:T(8,128)(2,1)} %fusion.27.own_in.other_in, bf16[2048,6144]{1,0:T(8,128)(2,1)} %all-gather.10.cloned.1.call-done), kind=kOutput, calls=%fused_computation.16 | convolution fusion | flops 51552190464 | bytes 83910656 | tf_op jit(solution)/shard_map/dot_general | solution.py:21
  196.9 78.6 %attn_fwd.1 = (bf16[2,1024,2048]{2,1,0:T(8,128)(2,1)}, bf16[2,1024,6144]{2,1,0:T(8,128)(2,1)}) custom-call(f32[2,1024,6144]{2,1,0:T(8,128)} %bitcast.129, f32[2,1024,128]{2,1,0:T(8,128)} %get-tuple-element.87.cos_ref, f32[2,1024,128]{2,1,0:T(8,128)} %get-tuple-element.88.sin_ref), custom_call_target="tpu_custom_call" | custom-call | flops 21474836480 | bytes 83886080 | tf_op jit(solution)/shard_map/attn_fwd/pallas_call | solution.py:121
  275.5 25.1 %fusion.23 = (f32[2048]{0:T(1024)S(1)}, bf16[2048,2048]{1,0:T(8,128)(2,1)}) fusion(bf16[2048,2048]{1,0:T(8,128)(2,1)} %bitcast.100, bf16[2048,2048]{1,0:T(8,128)(2,1)} %all-gather.12.cloned.1.call-done, bf16[2,1024,2048]{2,1,0:T(8,128)(2,1)} %param.15), kind=kOutput, calls=%fused_computation.35 | convolution fusion | flops 17205032960 | bytes 33562624 | tf_op jit(solution)/shard_map/dot_general | solution.py:21
  333.1 58.2 %fusion.32 = f32[2048,5504]{1,0:T(8,128)} fusion(bf16[2048,2048]{1,0:T(8,128)(2,1)} %fusion.20.own_in.other_in, bf16[2048,5504]{1,0:T(8,128)(2,1)} %all-gather.14.cloned.1.call-done), kind=kOutput, calls=%fused_computation.80 | convolution fusion | flops 46170898432 | bytes 76021760 | tf_op jit(solution)/shard_map/dot_general | solution.py:21
  405.3 66.4 %multiply_convert_fusion = (bf16[2048,5504]{1,0:T(8,128)(2,1)}, f32[2048,5504]{1,0:T(8,128)}) fusion(f32[2048,5504]{1,0:T(8,128)} %fusion.32, bf16[2048,2048]{1,0:T(8,128)(2,1)} %fusion.20.own_in.other_in, bf16[2048,5504]{1,0:T(8,128)(2,1)} %all-gather.16.cloned.1.call-done), kind=kOutput, calls=%fused_computation.7 | convolution fusion | flops 46238531584 | bytes 143654912 | tf_op jit(solution)/shard_map/dot_general | solution.py:21
  471.8 31.0 %fusion.33 = f32[5504,1024]{1,0:T(8,128)} fusion(bf16[2048,5504]{1,0:T(8,128)(2,1)} %get-tuple-element.54, bf16[2048,1024]{1,0:T(8,128)(2,1)} %get-tuple-element.45), kind=kOutput, calls=%fused_computation.81 | convolution fusion | flops 23085449216 | bytes 49283072 | tf_op jit(solution)/shard_map/dot_general | solution.py:29
  510.0 33.4 %convolution_add_fusion = f32[5504,1024]{1,0:T(8,128)} fusion(f32[5504,1024]{1,0:T(8,128)} %fusion.33, bf16[2048,5504]{1,0:T(8,128)(2,1)} %collective-permute-done.4, bf16[2048,1024]{1,0:T(8,128)(2,1)} %collective-permute-done.1), kind=kOutput, calls=%fused_computation.46 | convolution fusion | flops 23091085312 | bytes 71827456 | tf_op jit(solution)/shard_map/dot_general | solution.py:29
  543.3 84.0 %fusion.4 = (bf16[2048,5504]{1,0:T(8,128)(2,1)}, bf16[2048,5504]{1,0:T(8,128)(2,1)}) fusion(f32[2048,5504]{1,0:T(8,128)} %fusion.32, f32[2048,5504]{1,0:T(8,128)} %get-tuple-element.84, bf16[2048,2048]{1,0:T(8,128)(2,1)} %bitcast.99, bf16[5504,2048]{1,0:T(8,128)(2,1)} %all-gather.18.cloned.1.call-done), kind=kOutput, calls=%fused_computation.6 | convolution fusion | flops 46339981312 | bytes 166199296 | tf_op jit(solution)/shard_map/dot_general | solution.py:25
  627.8 34.6 %fusion.35 = f32[1024,5504]{1,0:T(8,128)} fusion(bf16[2048,1024]{1,0:T(8,128)(2,1)} %get-tuple-element.47, bf16[2048,5504]{1,0:T(8,128)(2,1)} %get-tuple-element.49), kind=kOutput, calls=%fused_computation.83 | convolution fusion | flops 23085449216 | bytes 49283072 | tf_op jit(solution)/shard_map/dot_general | solution.py:29
  662.3 34.5 %fusion.34 = f32[1024,5504]{1,0:T(8,128)} fusion(bf16[2048,1024]{1,0:T(8,128)(2,1)} %get-tuple-element.47, bf16[2048,5504]{1,0:T(8,128)(2,1)} %get-tuple-element.48), kind=kOutput, calls=%fused_computation.82 | convolution fusion | flops 23085449216 | bytes 49283072 | tf_op jit(solution)/shard_map/dot_general | solution.py:29
  696.9 35.1 %convolution_add_fusion.1 = f32[1024,5504]{1,0:T(8,128)} fusion(f32[1024,5504]{1,0:T(8,128)} %fusion.35, bf16[2048,1024]{1,0:T(8,128)(2,1)} %collective-permute-done.2, bf16[2048,5504]{1,0:T(8,128)(2,1)} %collective-permute-done.6), kind=kOutput, calls=%fused_computation.47 | convolution fusion | flops 23091085312 | bytes 71827456 | tf_op jit(solution)/shard_map/dot_general | solution.py:29
  732.0 35.2 %convolution_add_fusion.2 = f32[1024,5504]{1,0:T(8,128)} fusion(f32[1024,5504]{1,0:T(8,128)} %fusion.34, bf16[2048,1024]{1,0:T(8,128)(2,1)} %collective-permute-done.2, bf16[2048,5504]{1,0:T(8,128)(2,1)} %collective-permute-done.5), kind=kOutput, calls=%fused_computation.48 | convolution fusion | flops 23091085312 | bytes 71827456 | tf_op jit(solution)/shard_map/dot_general | solution.py:29
  767.3 60.2 %fusion.36 = f32[2048,2048]{1,0:T(8,128)} fusion(bf16[2048,5504]{1,0:T(8,128)(2,1)} %get-tuple-element.48, bf16[2048,5504]{1,0:T(8,128)(2,1)} %all-gather.14.cloned.1.call-done), kind=kOutput, calls=%fused_computation.84 | convolution fusion | flops 46170898432 | bytes 61865984 | tf_op jit(solution)/shard_map/dot_general | solution.py:25
  827.5 67.1 %fusion.22 = (f32[2048]{0:T(1024)}, f32[2048]{0:T(1024)S(1)}, bf16[2048,2048]{1,0:T(8,128)(2,1)}) fusion(bf16[2048,2048]{1,0:T(8,128)(2,1)} %get-tuple-element.82, f32[2048]{0:T(1024)S(1)} %copy-done.7, f32[2048]{0:T(1024)S(1)} %bitcast.114, f32[2048,2048]{1,0:T(8,128)} %fusion.36, bf16[2048,5504]{1,0:T(8,128)(2,1)} %get-tuple-element.49, ...), kind=kOutput, calls=%fused_computation.34 | convolution fusion | flops 46212841472 | bytes 78675968 | tf_op jit(solution)/shard_map/dot_general | solution.py:25
  960.3 126.3 %attn_bwd.1 = (bf16[2,1024,6144]{2,1,0:T(8,128)(2,1)}, f32[2,1,6144]{2,1,0:T(1,128)}) custom-call(bf16[2,1024,6144]{2,1,0:T(8,128)(2,1)} %get-tuple-element.41.rot_ref, bf16[2,1024,2048]{2,1,0:T(8,128)(2,1)} %bitcast.131, f32[2,1024,128]{2,1,0:T(8,128)} %get-tuple-element.87.cos_ref, f32[2,1024,128]{2,1,0:T(8,128)} %get-tuple-element.88.sin_ref), custom_call_target="tpu_custom_call" | custom-call | flops 53687091200 | bytes 58720256 | tf_op jit(solution)/shard_map/attn_bwd/pallas_call | solution.py:136
  1086.8 33.5 %fusion.38 = f32[1024,6144]{1,0:T(8,128)} fusion(bf16[2048,1024]{1,0:T(8,128)(2,1)} %get-tuple-element.53, bf16[2048,6144]{1,0:T(8,128)(2,1)} %bitcast.127), kind=kOutput, calls=%fused_computation.86 | convolution fusion | flops 25769803776 | bytes 54525952 | tf_op jit(solution)/shard_map/dot_general | solution.py:29
  1124.1 37.4 %convolution_add_fusion.3 = f32[1024,6144]{1,0:T(8,128)} fusion(f32[1024,6144]{1,0:T(8,128)} %fusion.38, bf16[2048,1024]{1,0:T(8,128)(2,1)} %collective-permute-done, bf16[2048,6144]{1,0:T(8,128)(2,1)} %collective-permute-done.8), kind=kOutput, calls=%fused_computation.49 | convolution fusion | flops 25776095232 | bytes 79691776 | tf_op jit(solution)/shard_map/dot_general | solution.py:29
  1180.7 72.9 %fusion.19 = (f32[2048]{0:T(1024)S(1)}, f32[2048]{0:T(1024)S(1)}, bf16[2048,2048]{1,0:T(8,128)(2,1)}) fusion(bf16[2,1024,2048]{2,1,0:T(8,128)(2,1)} %param.15, f32[2048]{0:T(1024)S(1)} %bitcast.111, f32[2048]{0:T(1024)S(1)} %bitcast.108, bf16[2048,6144]{1,0:T(8,128)(2,1)} %bitcast.128, bf16[2048,6144]{1,0:T(8,128)(2,1)} %all-gather.10.cloned.1.call-done), kind=kOutput, calls=%fused_computation.31 | convolution fusion | flops 51577356288 | bytes 67141632 | tf_op jit(solution)/shard_map/dot_general | solution.py:25
  1284.0 57.6 %fusion.24 = bf16[2048,2048]{1,0:T(8,128)(2,1)} fusion(bf16[2048,2048]{1,0:T(8,128)(2,1)} %get-tuple-element.82, bf16[2048,5504]{1,0:T(8,128)(2,1)} %get-tuple-element.54, bf16[5504,2048]{1,0:T(8,128)(2,1)} %all-gather.18.cloned.1.call-done), kind=kOutput, calls=%fused_computation.36 | convolution fusion | flops 46183481344 | bytes 61865984 | tf_op jit(solution)/shard_map/dot_general | solution.py:21
  1341.7 39.3 %reduce-scatter.6.cloned.1.call-done.in_ref = f32[256,6144]{1,0:T(8,128)} async-done(((f32[1024,6144]{1,0:T(8,128)}), f32[256,6144]{1,0:T(8,128)}) %reduce-scatter.6.cloned.1.call-update) | async-done | bytes 6291472 | tf_op jit(solution)/shard_map/reduce_scatter | solution.py:202
  1386.9 78.4 %reduce-scatter.8.cloned.1.call-done = f32[256,2048]{1,0:T(8,128)} async-done(((f32[1024,2048]{1,0:T(8,128)}), f32[256,2048]{1,0:T(8,128)}) %reduce-scatter.8.cloned.1.call-update) | async-done | bytes 2097168 | tf_op jit(solution)/shard_map/reduce_scatter | solution.py:202
  1465.3 198.6 %reduce-scatter.12.cloned.1.call-done = f32[256,5504]{1,0:T(8,128)} async-done(((f32[1024,5504]{1,0:T(8,128)}), f32[256,5504]{1,0:T(8,128)}) %reduce-scatter.12.cloned.1.call-update) | async-done | bytes 5636112 | tf_op jit(solution)/shard_map/reduce_scatter | solution.py:202
  1664.0 198.5 %reduce-scatter.10.cloned.1.call-done = f32[256,5504]{1,0:T(8,128)} async-done(((f32[1024,5504]{1,0:T(8,128)}), f32[256,5504]{1,0:T(8,128)}) %reduce-scatter.10.cloned.1.call-update) | async-done | bytes 5636112 | tf_op jit(solution)/shard_map/reduce_scatter | solution.py:202
  (112 shorter events, 239.7 us)
Async XLA Ops:
  7.2 126.9 %all-gather.10.cloned.1.call-start = ((), (), s32[]{:S(2)}) async-start(), calls=%async_computation.5 | async-start | bytes 28311552 | tf_op jit(solution)/shard_map/all_gather | solution.py:163
  11.4 264.1 %all-gather.12.cloned.1.call-start = ((), (), s32[]{:S(2)}) async-start(), calls=%async_computation.6 | async-start | bytes 9437184 | tf_op jit(solution)/shard_map/all_gather | solution.py:163
  12.1 321.0 %all-gather.14.cloned.1.call-start = ((), (), s32[]{:S(2)}) async-start(), calls=%async_computation.7 | async-start | bytes 25362432 | tf_op jit(solution)/shard_map/all_gather | solution.py:163
  12.9 392.4 %all-gather.16.cloned.1.call-start = ((), (), s32[]{:S(2)}) async-start(), calls=%async_computation.8 | async-start | bytes 25362432 | tf_op jit(solution)/shard_map/all_gather | solution.py:163
  13.4 529.9 %all-gather.18.cloned.1.call-start = ((), (), s32[]{:S(2)}) async-start(), calls=%async_computation.9 | async-start | bytes 25362432 | tf_op jit(solution)/shard_map/all_gather | solution.py:163
  49.9 13.9 collective-permute-start
  57.0 10.6 collective-permute-start.1
  275.5 25.7 %copy-start.4 = (f32[1,2,8,128]{3,1,2,0:T(2,128)S(1)}, f32[1,2,8,128]{3,1,2,0:T(2,128)}, u32[]{:S(2)}) copy-start(f32[1,2,8,128]{3,1,2,0:T(2,128)} %copy.34) | copy-start | bytes 24580
  318.2 7.6 collective-permute-start.2
  325.6 7.5 collective-permute-start.3
  325.8 837.9 %reduce-scatter.14.cloned.1.call-start = ((), (), s32[]{:S(2)}) async-start(), calls=%async_computation.14 | async-start | bytes 28180480 | tf_op jit(solution)/shard_map/reduce_scatter | solution.py:202
  471.7 38.3 %collective-permute-start.4 = (bf16[2048,5504]{1,0:T(8,128)(2,1)}, bf16[2048,5504]{1,0:T(8,128)(2,1)}, u32[]{:S(2)}, u32[]{:S(2)}) collective-permute-start(bf16[2048,5504]{1,0:T(8,128)(2,1)} %get-tuple-element.54), channel_id=1, source_target_pairs={{0,1},{1,0},{2,3},{3,2},{4,5},{5,4},{6,7},{7,6}} | collective-permute-start | bytes 67633160 | tf_op jit(solution)/shard_map/ppermute | solution.py:167
  627.3 69.6 %collective-permute-start.6 = (bf16[2048,5504]{1,0:T(8,128)(2,1)}, bf16[2048,5504]{1,0:T(8,128)(2,1)}, u32[]{:S(2)}, u32[]{:S(2)}) collective-permute-start(bf16[2048,5504]{1,0:T(8,128)(2,1)} %get-tuple-element.49), channel_id=1, source_target_pairs={{0,1},{1,0},{2,3},{3,2},{4,5},{5,4},{6,7},{7,6}} | collective-permute-start | bytes 67633160 | tf_op jit(solution)/shard_map/ppermute | solution.py:167
  627.4 104.6 %collective-permute-start.5 = (bf16[2048,5504]{1,0:T(8,128)(2,1)}, bf16[2048,5504]{1,0:T(8,128)(2,1)}, u32[]{:S(2)}, u32[]{:S(2)}) collective-permute-start(bf16[2048,5504]{1,0:T(8,128)(2,1)} %get-tuple-element.48), channel_id=1, source_target_pairs={{0,1},{1,0},{2,3},{3,2},{4,5},{5,4},{6,7},{7,6}} | collective-permute-start | bytes 67633160 | tf_op jit(solution)/shard_map/ppermute | solution.py:167
  767.3 60.2 %copy-start.5 = (f32[1,2,8,128]{3,1,2,0:T(2,128)S(1)}, f32[1,2,8,128]{3,1,2,0:T(2,128)}, u32[]{:S(2)}) copy-start(f32[1,2,8,128]{3,1,2,0:T(2,128)} %copy.34) | copy-start | bytes 24580
  767.3 60.2 %copy-start.7 = (f32[2048]{0:T(1024)S(1)}, f32[2048]{0:T(1024)}, u32[]{:S(2)}) copy-start(f32[2048]{0:T(1024)} %copy-done.6) | copy-start | bytes 24580
  907.7 37.3 %collective-permute-start.7 = (bf16[2048,2048]{1,0:T(8,128)(2,1)}, bf16[2048,2048]{1,0:T(8,128)(2,1)}, u32[]{:S(2)}, u32[]{:S(2)}) collective-permute-start(bf16[2048,2048]{1,0:T(8,128)(2,1)} %fusion.18), channel_id=1, source_target_pairs={{0,1},{1,0},{2,3},{3,2},{4,5},{5,4},{6,7},{7,6}} | collective-permute-start | bytes 25165832 | tf_op jit(solution)/shard_map/ppermute | solution.py:167
  907.9 473.1 %reduce-scatter.6.cloned.1.call-start = ((), (), s32[]{:S(2)}) async-start(), calls=%async_computation.10 | async-start | bytes 31457280 | tf_op jit(solution)/shard_map/reduce_scatter | solution.py:202
  1086.6 37.5 %collective-permute-start.8 = (bf16[2048,6144]{1,0:T(8,128)(2,1)}, bf16[2048,6144]{1,0:T(8,128)(2,1)}, u32[]{:S(2)}, u32[]{:S(2)}) collective-permute-start(bf16[2048,6144]{1,0:T(8,128)(2,1)} %bitcast.126), channel_id=1, source_target_pairs={{0,1},{1,0},{2,3},{3,2},{4,5},{5,4},{6,7},{7,6}} | collective-permute-start | bytes 75497480 | tf_op jit(solution)/shard_map/ppermute | solution.py:167
  1161.5 303.8 %reduce-scatter.8.cloned.1.call-start = ((), (), s32[]{:S(2)}) async-start(), calls=%async_computation.11 | async-start | bytes 10485760 | tf_op jit(solution)/shard_map/reduce_scatter | solution.py:202
  1162.3 501.7 %reduce-scatter.12.cloned.1.call-start = ((), (), s32[]{:S(2)}) async-start(), calls=%async_computation.13 | async-start | bytes 28180480 | tf_op jit(solution)/shard_map/reduce_scatter | solution.py:202
  1163.0 699.4 %reduce-scatter.10.cloned.1.call-start = ((), (), s32[]{:S(2)}) async-start(), calls=%async_computation.12 | async-start | bytes 28180480 | tf_op jit(solution)/shard_map/reduce_scatter | solution.py:202
  1167.9 5.3 collective-permute-start.9
  1180.7 72.9 %copy-start.10 = (f32[2048]{0:T(1024)S(1)}, f32[2048]{0:T(1024)}, u32[]{:S(2)}) copy-start(f32[2048]{0:T(1024)} %get-tuple-element.60) | copy-start | bytes 24580
  (7 other events, 91.2 us)
Sparse Core Ops, SparseCore 0:
  11.5 122.5 all-gather.9
  135.9 48.6 all-gather.11
  186.4 108.5 all-gather.13
  296.7 108.5 all-gather.15
  406.9 108.5 all-gather.17
  908.0 194.6 reduce-scatter.13
  1161.6 219.2 reduce-scatter.5
  1384.5 80.7 reduce-scatter.7
  1469.0 194.8 reduce-scatter.11
  1667.5 194.8 reduce-scatter.9
